TPU v7x, 32 devices: a whole 2x2x4 slice. The times are simulated.
32 devices in a mesh: grp: 2 (over y), seq: 4 (over z), head: 2 (over x), sub: 2 (over core).
Axes of the slice: x: 2, y: 2, z: 4, core: 2. Of those that a mesh axis runs over, the one named last changes fastest.
Arguments:
- latents: bfloat16 [8, 256, 1152], P(('grp', 'seq'), ('head', 'sub')), parts along dimension 0, may hold values from -6 to 6
- timestep: int32 [2], P('grp'), parts along dimension 0, may hold values from 0 to 29
- time_table: float32 [30, 3, 1152], replicated, may hold values from -3 to 3
- shift_table: float32 [2, 3, 1152], replicated, may hold values from -2 to 2
- qkv_weight: bfloat16 [2, 1152, 16, 216], P(None, None, ('head', 'sub')), may hold values from -0.1875 to 0.1875
- norm_gains: float32 [2, 2, 72], replicated, may hold values from 0.1 to 1.9
- out_weight: bfloat16 [2, 1152, 1152], P(None, ('head', 'sub')), may hold values from -0.1875 to 0.1875
Outputs:
- mixed: bfloat16 [8, 256, 1152], P(('grp', 'seq'), ('head', 'sub')), parts along dimension 0
There are 2 independent parts, one for each index of `grp`. A program takes and returns all parts, laid end to end along the dimension named above; an argument that names none is the same for every part. Nothing has to cross between parts.
All inputs are finite; a program needn't handle non-finite values.
Results may differ from a plain program's by a relative error of at most 0.0095.
Values may be sent and summed in bfloat16 or wider, within the bound.
No kernel may reach another device: no remote copies, remote signals or barrier semaphores. Data moves between devices by JAX's collectives and lax.ppermute only.
A program may use at most 64 MiB of HBM per device.

v0:
```python
import jax
import jax.numpy as jnp
from jax import lax
from jax.sharding import PartitionSpec as P

EPSILON = 1e-06


def modulate(values, shift_row, scale_row):
    widened = values.astype(jnp.float32)
    center = jnp.mean(widened, axis=-1, keepdims=True)
    spread = jnp.mean(jnp.square(widened - center), axis=-1, keepdims=True)
    normal = (widened - center) * lax.rsqrt(spread + EPSILON)
    return (normal * (1.0 + scale_row) + shift_row).astype(jnp.bfloat16)


def rms_gain(values, gain_row):
    return (
        values
        * lax.rsqrt(jnp.mean(jnp.square(values), axis=-1, keepdims=True) + EPSILON)
        * gain_row
    )


def project(normed, weight, gain_pair):
    leading = normed.shape[:-1]
    head_count = weight.shape[1]
    head_dim = weight.shape[2] // 3
    flattened = jnp.dot(
        normed.reshape(-1, normed.shape[-1]),
        weight.reshape(weight.shape[0], -1),
        preferred_element_type=jnp.float32,
    )
    pieces = flattened.reshape(leading + (head_count, 3, head_dim))
    queries = rms_gain(pieces[..., 0, :], gain_pair[0])
    key_part = rms_gain(pieces[..., 1, :], gain_pair[1])
    return jnp.concatenate([queries, key_part, pieces[..., 2, :]], axis=-1).astype(jnp.bfloat16)


def attend(packed):
    head_dim = packed.shape[-1] // 3
    queries = packed[..., :head_dim]
    key_part = packed[..., head_dim : 2 * head_dim]
    value_part = packed[..., 2 * head_dim :]
    count = queries.shape[0]
    block = 512 if count % 512 == 0 else count
    blocks = queries.reshape((count // block, block) + queries.shape[1:])

    def one_block(query_block):
        scores = jnp.einsum(
            "qhd,khd->hqk", query_block, key_part, preferred_element_type=jnp.float32
        ) * head_dim ** (-0.5)
        exponent = jnp.exp(scores)
        weights = (exponent / jnp.sum(exponent, axis=-1, keepdims=True)).astype(jnp.bfloat16)
        return jnp.einsum(
            "hqk,khd->qhd", weights, value_part, preferred_element_type=jnp.float32
        ).astype(jnp.bfloat16)

    result = lax.map(one_block, blocks)
    return result.reshape((count,) + result.shape[2:])


def body(latents, timestep, time_table, shift_table, qkv_weight, norm_gains, out_weight):
    feature_width = latents.shape[2]
    chosen = (jnp.arange(time_table.shape[0]) == timestep[0])[:, None, None]
    shared = jnp.sum(jnp.where(chosen, time_table, 0.0), axis=0)
    modulation = shared[None] + shift_table

    def gathered_heads(normed, layer_index):
        return project(
            lax.all_gather(normed, ("head", "sub"), axis=1, tiled=True),
            qkv_weight[layer_index],
            norm_gains[layer_index],
        )

    def back_to_tokens(attended, layer_index):
        merged = attended.reshape(attended.shape[0], attended.shape[1], -1)
        all_heads = lax.all_to_all(merged, ("head", "sub"), split_axis=1, concat_axis=2, tiled=True)
        row_block = all_heads.reshape(-1, all_heads.shape[-1])
        summed = jnp.dot(
            row_block,
            lax.all_gather(out_weight[layer_index], ("head", "sub"), axis=0, tiled=True),
            preferred_element_type=jnp.float32,
        )
        return summed.reshape(all_heads.shape[0], all_heads.shape[1], feature_width)

    normed = modulate(latents, modulation[0, 0], modulation[0, 1])
    packed = gathered_heads(normed, 0)
    attended = lax.map(attend, packed)
    update = back_to_tokens(attended, 0)
    current = (latents.astype(jnp.float32) + modulation[0, 2] * update).astype(jnp.bfloat16)
    shifted_rows = lax.all_to_all(current, "seq", split_axis=1, concat_axis=0, tiled=True)
    packed = gathered_heads(modulate(shifted_rows, modulation[1, 0], modulation[1, 1]), 1)
    attended = jax.vmap(attend, in_axes=1, out_axes=1)(packed)
    update = back_to_tokens(attended, 1)
    result = (shifted_rows.astype(jnp.float32) + modulation[1, 2] * update).astype(jnp.bfloat16)
    return lax.all_to_all(result, "seq", split_axis=0, concat_axis=1, tiled=True)


def solution(mesh):
    return jax.shard_map(
        body,
        mesh=mesh,
        in_specs=(
            P(("grp", "seq"), ("head", "sub"), None),
            P("grp"),
            P(),
            P(),
            P(None, None, ("head", "sub"), None),
            P(),
            P(None, ("head", "sub"), None),
        ),
        out_specs=P(("grp", "seq"), ("head", "sub"), None),
        check_vma=False,
    )
```

profile of v0, /device:TPU:0, one launch (start us, length us, event | category | flops | bytes accessed | tf_op | source)
XLA Modules:
  0.0 99.6 jit_solution(3621725734920662956)
XLA Ops:
  6.5 2.5 %fusion.61 = (bf16[1,288,1152]{2,1,0:T(8,128)(2,1)}, bf16[1,288,1152]{2,1,0:T(8,128)(2,1)}) fusion(bf16[2,288,1152]{2,1,0:T(8,128)(2,1)} %param.13), kind=kLoop, calls=%fused_computation.89 | loop fusion | bytes 2654208 | tf_op jit(solution)/shard_map/slice | solution.py:82
  9.8 0.1 select_reduce_fusion
  10.0 0.1 convert_reduce_fusion
  10.2 0.2 fusion.33
  10.4 0.1 fusion.36
  10.5 9.0 %all_gather.12 = bf16[1,256,1152]{2,1,0:T(8,128)(2,1)S(1)} all-gather(bf16[1,64,1152]{2,1,0:T(8,128)(2,1)S(1)} %fusion.36), channel_id=1, replica_groups=mesh['grp'=2,'seq'=4,'head'=2,'sub'=2] {'head','sub'}, dimensions={1}, use_global_device_ids=true | all-gather | bytes 737280 | tf_op jit(solution)/shard_map/all_gather | solution.py:71
  19.5 4.1 %fusion.60 = (bf16[1,1152,4,216]{1,3,2,0:T(8,128)(2,1)}, bf16[1,1152,4,216]{1,3,2,0:T(8,128)(2,1)S(1)}) fusion(bf16[2,1152,4,216]{1,3,2,0:T(8,128)(2,1)} %param.11), kind=kLoop, calls=%fused_computation.88 | loop fusion | bytes 7962624 | tf_op jit(solution)/shard_map/slice | solution.py:72
  23.6 0.8 convolution_bitcast_fusion
  24.5 0.4 fusion.25
  24.9 0.3 convolution_convert_fusion.1
  25.3 0.4 copy.35
  25.7 0.5 broadcast.178
  26.2 1.9 %reduce.20 = bf16[256,288]{1,0:T(8,128)(2,1)S(1)} reduce(bf16[256,1,288]{2,1,0:T(2,128)(2,1)S(1)} %bitcast.139, bf16[]{:T(256)} %broadcast.178), dimensions={1}, to_apply=%bitcast.118.reduce_sub_computation | reduce | bytes 294914
  28.1 0.3 reshape.234
  28.4 9.1 %all_to_all.51 = bf16[4,2,9216]{2,1,0:T(2,128)(2,1)S(1)} all-to-all(bf16[4,2,9216]{2,1,0:T(2,128)(2,1)S(1)} %reshape.234), channel_id=1, replica_groups=mesh['grp'=2,'seq'=4,'head'=2,'sub'=2] {'head','sub'}, dimensions={0} | all-to-all | bytes 294912 | tf_op jit(solution)/shard_map/all_to_all | solution.py:78
  37.5 0.4 reshape.235
  37.9 0.2 copy.36
  38.0 0.2 reshape.218
  38.2 1.1 %all-gather.5.cloned.1.call-done = bf16[1,1152,1152]{2,1,0:T(8,128)(2,1)} async-done(((bf16[1,288,1152]{2,1,0:T(8,128)(2,1)}), bf16[1,1152,1152]{2,1,0:T(8,128)(2,1)}) %all-gather.5.cloned.1.call-update) | async-done | bytes 2654224 | tf_op jit(solution)/shard_map/all_gather | solution.py:82
  39.3 2.3 %fusion.19 = bf16[1,64,1152]{2,1,0:T(8,128)(2,1)S(1)} fusion(bf16[64,1152]{1,0:T(8,128)(2,1)S(1)} %reshape.218, bf16[1,1152,1152]{2,1,0:T(8,128)(2,1)} %all-gather.5.cloned.1.call-done, bf16[1,64,1152]{2,1,0:T(8,128)(2,1)S(1)} %copy-done, f32[1152]{0:T(1024)S(1)} %get-tuple-element.58), kind=kOutput, calls=%fused_computation.9 | convolution fusion | flops 170164224 | bytes 3101184 | tf_op jit(solution)/shard_map/dot_general | solution.py:80
  41.6 0.2 copy.61
  41.9 1.5 %reduce.21 = bf16[64,1152]{1,0:T(8,128)(2,1)S(1)} reduce(bf16[64,1,1152]{2,1,0:T(2,128)(2,1)S(1)} %bitcast.140, bf16[]{:T(256)} %broadcast.178), dimensions={1}, to_apply=%bitcast.131.reduce_sub_computation | reduce | bytes 294914
  43.4 0.7 reshape.236
  44.1 4.6 %all-to-all-start.1 = ((bf16[4,2,9216]{2,1,0:T(2,128)(2,1)}), bf16[4,2,9216]{2,1,0:T(2,128)(2,1)S(1)}, u32[]{:S(2)}, u32[]{:S(2)}) async-start(bf16[4,2,9216]{2,1,0:T(2,128)(2,1)} %reshape.236), calls=%async_computation.1 | async-start | bytes 294912 | tf_op jit(solution)/shard_map/all_to_all | solution.py:92
  48.7 0.7 all-gather.7.cloned.1.call-update
  49.4 5.8 %all-to-all-done.1 = bf16[4,2,9216]{2,1,0:T(2,128)(2,1)S(1)} async-done(((bf16[4,2,9216]{2,1,0:T(2,128)(2,1)}), bf16[4,2,9216]{2,1,0:T(2,128)(2,1)S(1)}, u32[]{:S(2)}, u32[]{:S(2)}) %all-to-all-start.1) | async-done | bytes 147488 | tf_op jit(solution)/shard_map/all_to_all | solution.py:92
  55.2 0.1 reshape.237
  55.3 0.6 convert_reduce_fusion.1
  55.9 0.1 div.61
  56.0 1.0 %multiply_reduce_fusion.2 = f32[64]{0:T(128)S(1)} fusion(f32[64]{0:T(128)S(1)} %broadcast_multiply_fusion, bf16[64,1,1152]{2,1,0:T(2,128)(2,1)S(1)} %reshape.237), kind=kLoop, calls=%fused_computation.46 | loop fusion | flops 294848 | bytes 147968 | tf_op jit(solution)/shard_map/reduce_sum | solution.py:12
  57.0 0.1 rsqrt.55
  57.1 0.1 add_convert_fusion
  57.2 9.7 %all_gather.14 = bf16[4,64,1152]{2,1,0:T(8,128)(2,1)S(1)} all-gather(bf16[4,16,1152]{2,1,0:T(8,128)(2,1)S(1)} %add_convert_fusion), channel_id=1, replica_groups=mesh['grp'=2,'seq'=4,'head'=2,'sub'=2] {'head','sub'}, dimensions={1}, use_global_device_ids=true | all-gather | bytes 737280 | tf_op jit(solution)/shard_map/all_gather | solution.py:71
  66.9 2.8 %fusion.27 = f32[4,64,4,3,72]{4,1,3,2,0:T(8,128)S(1)} fusion(bf16[4,3,72,1152,1]{3,2,1,0,4:T(8,128)(2,1)} %bitcast.137, bf16[4,64,1152]{2,1,0:T(8,128)(2,1)S(1)} %all_gather.14), kind=kOutput, calls=%fused_computation.18 | convolution fusion | flops 509607936 | bytes 3465216 | tf_op jit(solution)/shard_map/dot_general | solution.py:29
  69.7 0.4 multiply_reduce_fusion.1
  70.1 0.3 fusion.41
  70.5 0.5 fusion.45
  70.9 0.3 copy.40
  71.3 0.3 copy.42
  71.7 0.4 fusion.26
  72.1 0.1 copy.50
  72.2 0.2 reshape.227
  72.5 7.9 %all_to_all.52 = bf16[4,64,288]{2,0,1:T(4,128)(2,1)S(1)} all-to-all(bf16[4,64,288]{2,0,1:T(4,128)(2,1)S(1)} %reshape.227), channel_id=1, replica_groups=mesh['grp'=2,'seq'=4,'head'=2,'sub'=2] {'head','sub'}, dimensions={1} | all-to-all | bytes 294912 | tf_op jit(solution)/shard_map/all_to_all | solution.py:78
  80.4 0.1 copy.46
  80.5 0.2 dot_general.54
  80.7 2.3 %fusion.22 = bf16[4,16,1152]{2,1,0:T(8,128)(2,1)S(1)} fusion(f32[4,16,1152]{2,1,0:T(8,128)S(1)} %bitcast.136, bf16[4,16,1152]{2,1,0:T(8,128)(2,1)S(1)} %dot_general.54, bf16[1,1152,1152]{2,1,0:T(8,128)(2,1)} %all-gather.7.cloned.1.call-done, f32[1152]{0:T(1024)S(1)} %get-tuple-element.46), kind=kOutput, calls=%fused_computation.10 | convolution fusion | flops 170090496 | bytes 3248640 | tf_op jit(solution)/shard_map/dot_general | solution.py:80
  83.0 9.0 %all_to_all.53 = bf16[4,16,1152]{2,1,0:T(8,128)(2,1)S(1)} all-to-all(bf16[4,16,1152]{2,1,0:T(8,128)(2,1)S(1)} %fusion.22), channel_id=1, replica_groups=mesh['grp'=2,'seq'=4,'head'=2,'sub'=2] {'seq'}, dimensions={0} | all-to-all | bytes 294912 | tf_op jit(solution)/shard_map/all_to_all | solution.py:97
  92.1 0.7 copy.64
  (30 shorter events, 0.5 us)
Async XLA Ops:
  6.5 3.2 %copy-start.1 = (f32[30,3,1152]{2,0,1:T(8,128)S(1)}, f32[30,3,1152]{2,0,1:T(8,128)}, u32[]{:S(2)}) copy-start(f32[30,3,1152]{2,0,1:T(8,128)} %param.9) | copy-start | bytes 1244164
  6.5 3.4 %copy-start.2 = (f32[2,3,1152]{2,0,1:T(2,128)S(1)}, f32[2,3,1152]{2,0,1:T(2,128)}, u32[]{:S(2)}) copy-start(f32[2,3,1152]{2,0,1:T(2,128)} %param.10) | copy-start | bytes 82948
  6.5 3.5 %copy-start = (bf16[1,64,1152]{2,1,0:T(8,128)(2,1)S(1)}, bf16[1,64,1152]{2,1,0:T(8,128)(2,1)}, u32[]{:S(2)}) copy-start(bf16[1,64,1152]{2,1,0:T(8,128)(2,1)} %param.7) | copy-start | bytes 442372
  6.5 32.7 %all-gather.5.cloned.1.call-start = ((), (), s32[]{:S(2)}) async-start(), calls=%async_computation.4 | async-start | bytes 3317760 | tf_op jit(solution)/shard_map/all_gather | solution.py:82
  23.6 0.9 copy-start.3
  44.1 11.1 %all-to-all-start.1 = ((bf16[4,2,9216]{2,1,0:T(2,128)(2,1)}), bf16[4,2,9216]{2,1,0:T(2,128)(2,1)S(1)}, u32[]{:S(2)}, u32[]{:S(2)}) async-start(bf16[4,2,9216]{2,1,0:T(2,128)(2,1)} %reshape.236), calls=%async_computation.1 | async-start | bytes 294912 | tf_op jit(solution)/shard_map/all_to_all | solution.py:92
  48.7 32.0 %all-gather.7.cloned.1.call-start = ((), (), s32[]{:S(2)}) async-start(), calls=%async_computation.5 | async-start | bytes 3317760 | tf_op jit(solution)/shard_map/all_gather | solution.py:82
Sparse Core Ops, SparseCore 0:
  9.2 30.0 all-gather.4
  51.0 27.7 all-gather.6
where the time goes:
time: 100 us; the launch traced here: 99.6 us
  blocking collectives  44.7 us (45%)
  between operations  14.3 us (14%)
  local copies, waits for them, and re-layouts  11.8 us (12%)
  matrix products  9.85 us (10%)
  waiting for transfers between devices  7.63 us (8%)
  other arithmetic  6.69 us (7%)
  starting transfers between devices  4.6 us (5%)
    all_gather x2, blocking collectives, gathered_heads(): lax.all_gather(normed, ('head', 'sub'), axis=1, tiled=True)  18.7 us
    all_to_all x2, blocking collectives, back_to_tokens(): lax.all_to_all(merged, ('head', 'sub'), split_axis=1, concat_axis=2, tile...  16.9 us
    all_to_all x1, blocking collectives, body(): lax.all_to_all(result, 'seq', split_axis=0, concat_axis=1, tiled=True)  9.04 us
    all_to_all x1, waiting for transfers between devices, body(): lax.all_to_all(current, 'seq', split_axis=1, concat_axis=0, tiled=True)  5.79 us
    dot_general x2, matrix products, back_to_tokens(): jnp.dot(row_block, lax.all_gather(out_weight[layer_index], ('head', 'sub'...  4.66 us
    all_to_all x1, starting transfers between devices, body(): lax.all_to_all(current, 'seq', split_axis=1, concat_axis=0, tiled=True)  4.6 us
    slice x1, local copies, waits for them, and re-layouts, gathered_heads(): qkv_weight[layer_index]  4.09 us
    dot_general x2, matrix products, project(): jnp.dot(normed.reshape(-1, normed.shape[-1]), weight.reshape(weight.shape...  3.56 us
  transfers between devices with their start and end apart: 3, of which 2 were waited for; matrix products, arithmetic and copies ran while one was open for 18% of the time, Pallas kernels for 0%

commit v1 on v0

--- a/solution.py
+++ b/solution.py
@@ -89,7 +89,10 @@
     attended = lax.map(attend, packed)
     update = back_to_tokens(attended, 0)
     current = (latents.astype(jnp.float32) + modulation[0, 2] * update).astype(jnp.bfloat16)
-    shifted_rows = lax.all_to_all(current, "seq", split_axis=1, concat_axis=0, tiled=True)
+    shifted_rows = jnp.concatenate(
+        lax.all_to_all(jnp.stack(jnp.split(current, lax.axis_size("seq"), axis=1)), "seq", 0, 0),
+        axis=0,
+    )
     packed = gathered_heads(modulate(shifted_rows, modulation[1, 0], modulation[1, 1]), 1)
     attended = jax.vmap(attend, in_axes=1, out_axes=1)(packed)
     update = back_to_tokens(attended, 1)

time: 100 us -> 94.8 us (0.948)
  blocking collectives: 44.7 us -> 47.7 us
  other arithmetic: 6.69 us -> 3.92 us
  waiting for transfers between devices: 7.63 us -> 5.24 us
  matrix products: 9.85 us -> 8.42 us
  starting transfers between devices: 4.6 us -> 3.38 us
    all_to_all x0 -> x1, blocking collectives: none -> 11.1 us  [body(): lax.all_to_all(jnp.stack(jnp.split(current, lax.axis_size('seq'), axis=1)...]
    all_to_all x2 -> x1, blocking collectives: 16.9 us -> 7.67 us  [back_to_tokens(): lax.all_to_all(merged, ('head', 'sub'), split_axis=1, concat_axis=2, tile...]
    dot_general x2, matrix products: 3.56 us -> 1.98 us  [project(): jnp.dot(normed.reshape(-1, normed.shape[-1]), weight.reshape(weight.shape...]
    unnamed x2 -> x1, other arithmetic: 3.37 us -> 1.88 us
    all_to_all x1, waiting for transfers between devices: 5.79 us -> 4.48 us  [back_to_tokens(): lax.all_to_all(merged, ('head', 'sub'), split_axis=1, concat_axis=2, tile...]
    all_to_all x1, starting transfers between devices: 4.6 us -> 3.34 us  [back_to_tokens(): lax.all_to_all(merged, ('head', 'sub'), split_axis=1, concat_axis=2, tile...]
    all_gather x2, blocking collectives: 18.7 us -> 19.9 us  [gathered_heads(): lax.all_gather(normed, ('head', 'sub'), axis=1, tiled=True)]
    all_gather x2, waiting for transfers between devices: 1.1 us -> 0.04 us  [back_to_tokens(): lax.all_gather(out_weight[layer_index], ('head', 'sub'), axis=0, tiled=True)]
  transfers between devices with their start and end apart: 3 -> 3, of which waited for: 2 -> 1; matrix products, arithmetic and copies ran while one was open for 18% -> 19% of each run, Pallas kernels for 0% -> 0%
where the time goes in v1:
time: 94.8 us; the launch traced here: 94.4 us
  blocking collectives  47.7 us (50%)
  between operations  14.4 us (15%)
  local copies, waits for them, and re-layouts  11.3 us (12%)
  matrix products  8.42 us (9%)
  waiting for transfers between devices  5.24 us (6%)
  other arithmetic  3.92 us (4%)
  starting transfers between devices  3.38 us (4%)
    all_gather x2, blocking collectives, gathered_heads(): lax.all_gather(normed, ('head', 'sub'), axis=1, tiled=True)  19.9 us
    all_to_all x1, blocking collectives, body(): lax.all_to_all(jnp.stack(jnp.split(current, lax.axis_size('seq'), axis=1)...  11.1 us
    all_to_all x1, blocking collectives, body(): lax.all_to_all(result, 'seq', split_axis=0, concat_axis=1, tiled=True)  9.04 us
    all_to_all x1, blocking collectives, back_to_tokens(): lax.all_to_all(merged, ('head', 'sub'), split_axis=1, concat_axis=2, tile...  7.67 us
    dot_general x2, matrix products, back_to_tokens(): jnp.dot(row_block, lax.all_gather(out_weight[layer_index], ('head', 'sub'...  4.81 us
    all_to_all x1, waiting for transfers between devices, back_to_tokens(): lax.all_to_all(merged, ('head', 'sub'), split_axis=1, concat_axis=2, tile...  4.48 us
    slice x1, local copies, waits for them, and re-layouts, gathered_heads(): qkv_weight[layer_index]  4.16 us
    all_to_all x1, starting transfers between devices, back_to_tokens(): lax.all_to_all(merged, ('head', 'sub'), split_axis=1, concat_axis=2, tile...  3.34 us
  transfers between devices with their start and end apart: 3, of which 1 were waited for; matrix products, arithmetic and copies ran while one was open for 19% of the time, Pallas kernels for 0%

profile of v1, /device:TPU:0, one launch (start us, length us, event | category | flops | bytes accessed | tf_op | source)
XLA Modules:
  0.0 94.4 jit_solution(3590001869496292245)
XLA Ops:
  6.5 2.6 %fusion.68 = (bf16[1,288,1152]{2,1,0:T(8,128)(2,1)}, bf16[1,288,1152]{2,1,0:T(8,128)(2,1)}) fusion(bf16[2,288,1152]{2,1,0:T(8,128)(2,1)} %param.13), kind=kLoop, calls=%fused_computation.100 | loop fusion | bytes 2654208 | tf_op jit(solution)/shard_map/slice | solution.py:82
  9.1 0.0 all-gather.5.cloned.1.call-update
  9.8 0.1 select_reduce_fusion
  10.0 0.1 slice_reduce_fusion.1
  10.1 0.1 convert_reduce_fusion
  10.2 0.2 fusion.36
  10.4 0.1 fusion.39
  10.6 9.0 %all_gather.12 = bf16[1,256,1152]{2,1,0:T(8,128)(2,1)S(1)} all-gather(bf16[1,64,1152]{2,1,0:T(8,128)(2,1)S(1)} %fusion.39), channel_id=1, replica_groups=mesh['grp'=2,'seq'=4,'head'=2,'sub'=2] {'head','sub'}, dimensions={1}, use_global_device_ids=true | all-gather | bytes 737280 | tf_op jit(solution)/shard_map/all_gather | solution.py:71
  19.6 4.2 %fusion.67 = (bf16[1,1152,4,216]{1,3,2,0:T(8,128)(2,1)S(1)}, bf16[1,1152,4,216]{1,3,2,0:T(8,128)(2,1)}) fusion(bf16[2,1152,4,216]{1,3,2,0:T(8,128)(2,1)} %param.11), kind=kLoop, calls=%fused_computation.99 | loop fusion | bytes 7962624 | tf_op jit(solution)/shard_map/slice | solution.py:72
  23.7 0.8 convolution_bitcast_fusion
  24.5 0.1 multiply_reduce_fusion.3
  24.6 0.0 copy-done.4
  24.6 0.4 fusion.25
  25.0 0.3 convolution_convert_fusion.1
  25.4 0.4 copy.34
  25.8 0.5 broadcast.174
  26.3 1.9 %reduce.19 = bf16[256,288]{1,0:T(8,128)(2,1)S(1)} reduce(bf16[256,1,288]{2,1,0:T(2,128)(2,1)S(1)} %bitcast.155, bf16[]{:T(256)} %broadcast.174), dimensions={1}, to_apply=%bitcast.143.reduce_sub_computation | reduce | bytes 294914
  28.2 1.0 %reshape.220 = bf16[4,2,9216]{2,1,0:T(2,128)(2,1)} reshape(bf16[256,288]{1,0:T(8,128)(2,1)S(1)} %reduce.19) | data formatting | bytes 294912
  29.2 3.3 %all-to-all-start = ((bf16[4,2,9216]{2,1,0:T(2,128)(2,1)}), bf16[4,2,9216]{2,1,0:T(2,128)(2,1)S(1)}, u32[]{:S(2)}, u32[]{:S(2)}) async-start(bf16[4,2,9216]{2,1,0:T(2,128)(2,1)} %reshape.220), calls=%async_computation | async-start | bytes 294912 | tf_op jit(solution)/shard_map/all_to_all | solution.py:78
  32.5 0.0 all-gather.7.cloned.1.call-start
  32.6 0.7 all-gather.7.cloned.1.call-update
  33.3 4.5 %all-to-all-done = bf16[4,2,9216]{2,1,0:T(2,128)(2,1)S(1)} async-done(((bf16[4,2,9216]{2,1,0:T(2,128)(2,1)}), bf16[4,2,9216]{2,1,0:T(2,128)(2,1)S(1)}, u32[]{:S(2)}, u32[]{:S(2)}) %all-to-all-start) | async-done | bytes 147488 | tf_op jit(solution)/shard_map/all_to_all | solution.py:78
  37.8 0.4 reshape.221
  38.2 0.2 copy.35
  38.3 0.2 reshape.205
  38.5 0.0 all-gather.5.cloned.1.call-done
  38.5 2.5 %fusion.19 = bf16[1,64,1152]{2,1,0:T(8,128)(2,1)S(1)} fusion(bf16[64,1152]{1,0:T(8,128)(2,1)S(1)} %reshape.205, bf16[1,1152,1152]{2,1,0:T(8,128)(2,1)} %all-gather.5.cloned.1.call-done, bf16[1,64,1152]{2,1,0:T(8,128)(2,1)S(1)} %copy-done, f32[1152]{0:T(1024)S(1)} %get-tuple-element.58), kind=kOutput, calls=%fused_computation.9 | convolution fusion | flops 170164224 | bytes 3101184 | tf_op jit(solution)/shard_map/dot_general | solution.py:80
  41.1 11.1 %all_to_all.47 = bf16[4,1,16,1152]{3,2,1,0:T(8,128)(2,1)S(1)} all-to-all(bf16[4,1,16,1152]{3,2,1,0:T(8,128)(2,1)S(1)} %pad_maximum_fusion), channel_id=1, replica_groups=mesh['grp'=2,'seq'=4,'head'=2,'sub'=2] {'seq'}, dimensions={0} | all-to-all | bytes 294912 | tf_op jit(solution)/shard_map/all_to_all | solution.py:93
  52.1 0.1 convert_reduce_fusion.1
  52.3 0.2 fusion.40
  52.4 0.1 fusion.43
  52.6 10.9 %all_gather.14 = bf16[4,64,1152]{2,1,0:T(8,128)(2,1)S(1)} all-gather(bf16[4,16,1152]{2,1,0:T(8,128)(2,1)S(1)} %fusion.43), channel_id=1, replica_groups=mesh['grp'=2,'seq'=4,'head'=2,'sub'=2] {'head','sub'}, dimensions={1}, use_global_device_ids=true | all-gather | bytes 737280 | tf_op jit(solution)/shard_map/all_gather | solution.py:71
  63.5 1.2 %fusion.27 = f32[4,64,4,3,72]{4,1,3,2,0:T(8,128)S(1)} fusion(bf16[4,3,72,1152,1]{3,2,1,0,4:T(8,128)(2,1)S(1)} %bitcast.153, bf16[4,64,1152]{2,1,0:T(8,128)(2,1)S(1)} %all_gather.14), kind=kOutput, calls=%fused_computation.18 | convolution fusion | flops 509607936 | bytes 3465216 | tf_op jit(solution)/shard_map/dot_general | solution.py:29
  64.7 0.4 multiply_reduce_fusion.1
  65.1 0.3 fusion.48
  65.5 0.5 fusion.52
  65.9 0.3 copy.38
  66.3 0.3 copy.40
  66.7 0.4 fusion.26
  67.1 0.1 copy.48
  67.2 0.2 reshape.213
  67.5 7.7 %all_to_all.48 = bf16[4,64,288]{2,0,1:T(4,128)(2,1)S(1)} all-to-all(bf16[4,64,288]{2,0,1:T(4,128)(2,1)S(1)} %reshape.213), channel_id=1, replica_groups=mesh['grp'=2,'seq'=4,'head'=2,'sub'=2] {'head','sub'}, dimensions={1} | all-to-all | bytes 294912 | tf_op jit(solution)/shard_map/all_to_all | solution.py:78
  75.2 0.1 copy.44
  75.3 0.2 dot_general.54
  75.4 0.0 all-gather.7.cloned.1.call-done
  75.5 2.3 %fusion.22 = bf16[4,16,1152]{2,1,0:T(8,128)(2,1)S(1)} fusion(bf16[4,16,1152]{2,1,0:T(8,128)(2,1)S(1)} %dot_general.54, bf16[1,1152,1152]{2,1,0:T(8,128)(2,1)} %all-gather.7.cloned.1.call-done, bf16[4,1,16,1152]{3,2,1,0:T(8,128)(2,1)S(1)} %all_to_all.47, f32[1152]{0:T(1024)S(1)} %get-tuple-element.46), kind=kOutput, calls=%fused_computation.10 | convolution fusion | flops 170164224 | bytes 3101184 | tf_op jit(solution)/shard_map/dot_general | solution.py:80
  77.8 9.0 %all_to_all.49 = bf16[4,16,1152]{2,1,0:T(8,128)(2,1)S(1)} all-to-all(bf16[4,16,1152]{2,1,0:T(8,128)(2,1)S(1)} %fusion.22), channel_id=1, replica_groups=mesh['grp'=2,'seq'=4,'head'=2,'sub'=2] {'seq'}, dimensions={0} | all-to-all | bytes 294912 | tf_op jit(solution)/shard_map/all_to_all | solution.py:100
  86.8 0.7 copy.59
  (27 shorter events, 0.3 us)
Async XLA Ops:
  6.5 3.3 %copy-start.2 = (f32[30,3,1152]{2,0,1:T(8,128)S(1)}, f32[30,3,1152]{2,0,1:T(8,128)}, u32[]{:S(2)}) copy-start(f32[30,3,1152]{2,0,1:T(8,128)} %param.9) | copy-start | bytes 1244164
  6.5 3.4 %copy-start.3 = (f32[2,3,1152]{2,0,1:T(2,128)S(1)}, f32[2,3,1152]{2,0,1:T(2,128)}, u32[]{:S(2)}) copy-start(f32[2,3,1152]{2,0,1:T(2,128)} %param.10) | copy-start | bytes 82948
  6.5 3.5 %copy-start = (bf16[1,64,1152]{2,1,0:T(8,128)(2,1)S(1)}, bf16[1,64,1152]{2,1,0:T(8,128)(2,1)}, u32[]{:S(2)}) copy-start(bf16[1,64,1152]{2,1,0:T(8,128)(2,1)} %param.7) | copy-start | bytes 442372
  6.5 32.0 %all-gather.5.cloned.1.call-start = ((), (), s32[]{:S(2)}) async-start(), calls=%async_computation.4 | async-start | bytes 3317760 | tf_op jit(solution)/shard_map/all_gather | solution.py:82
  23.7 0.9 copy-start.4
  29.2 8.6 %all-to-all-start = ((bf16[4,2,9216]{2,1,0:T(2,128)(2,1)}), bf16[4,2,9216]{2,1,0:T(2,128)(2,1)S(1)}, u32[]{:S(2)}, u32[]{:S(2)}) async-start(bf16[4,2,9216]{2,1,0:T(2,128)(2,1)} %reshape.220), calls=%async_computation | async-start | bytes 294912 | tf_op jit(solution)/shard_map/all_to_all | solution.py:78
  32.5 42.9 %all-gather.7.cloned.1.call-start = ((), (), s32[]{:S(2)}) async-start(), calls=%async_computation.5 | async-start | bytes 3317760 | tf_op jit(solution)/shard_map/all_gather | solution.py:82
  38.5 25.0 %copy-start.1 = (bf16[1,1152,4,216]{1,3,2,0:T(8,128)(2,1)S(1)}, bf16[1,1152,4,216]{1,3,2,0:T(8,128)(2,1)}, u32[]{:S(2)}) copy-start(bf16[1,1152,4,216]{1,3,2,0:T(8,128)(2,1)} %get-tuple-element.60) | copy-start | bytes 5971972
Sparse Core Ops, SparseCore 0:
  9.3 28.9 all-gather.4
  39.8 28.8 all-gather.6
